TPU v7x, 32 devices: a whole 2x2x4 slice. The times are simulated.
32 devices in a mesh: dp: 8 (over y, x, core), tensor: 4 (over z).
Axes of the slice: x: 2, y: 2, z: 4, core: 2. Of those that a mesh axis runs over, the one named last changes fastest.
Arguments:
- teacher_in: bfloat16 [2048, 2048], P('dp'), may hold values from -13 to 13
- teacher_gain: float32 [2, 2048], replicated, may hold values from 0.25 to 1.75
- t_gate: bfloat16 [2, 2048, 5472], P(None, 'dp', 'tensor'), may hold values from -0.125 to 0.125
- t_up: bfloat16 [2, 2048, 5472], P(None, 'dp', 'tensor'), may hold values from -0.125 to 0.125
- t_down: bfloat16 [2, 5472, 2048], P(None, 'tensor', 'dp'), may hold values from -0.078125 to 0.078125
- student_in: bfloat16 [2048, 1024], P('dp'), may hold values from -13 to 13
- student_gain: float32 [2, 1024], replicated, may hold values from 0.3 to 3.5
- s_gate: bfloat16 [2, 1024, 4096], P(None, None, 'tensor'), may hold values from -0.1875 to 0.1875
- s_up: bfloat16 [2, 1024, 4096], P(None, None, 'tensor'), may hold values from -0.1875 to 0.1875
- s_down: bfloat16 [2, 4096, 1024], P(None, 'tensor'), may hold values from -0.09375 to 0.09375
- proj: bfloat16 [1024, 2048], P(None, 'tensor'), may hold values from -1 to 1
- layer_map: int32 [2], replicated, may hold values from 0 to 1, each once
Outputs:
- teacher_states: bfloat16 [2, 2048, 2048], P(None, ('dp', 'tensor'))
- grad_gate: float32 [2, 1024, 4096], P(None, 'dp', 'tensor')
- grad_up: float32 [2, 1024, 4096], P(None, 'dp', 'tensor')
- grad_down: float32 [2, 4096, 1024], P(None, 'tensor', 'dp')
- grad_proj: float32 [1024, 2048], P('dp', 'tensor')
- mean_error: float32 [2], replicated
- grad_rms: float32 [4], replicated
Inputs may be any that keep to these rules, and one draw needn't show every extreme that they name: `layer_map`: each teacher sublayer is matched to exactly one student sublayer.
All inputs are finite; a program needn't handle non-finite values.
Results may differ from a plain program's by a relative error of at most 0.02.
Values may be sent and summed in bfloat16 or wider, within the bound.
No kernel may reach another device: no remote copies, remote signals or barrier semaphores. Data moves between devices by JAX's collectives and lax.ppermute only.
A program may use at most 128 MiB of HBM per device.

v0:
```python
import jax
import jax.numpy as jnp
from jax import lax
from jax.sharding import PartitionSpec as P

DT = 2048
DS = 1024
FS = 4096
T_LAYERS = 2
S_LAYERS = 2
SEQ = 512
EPSILON = 1e-05


def inverse_rms(values):
    return lax.rsqrt(jnp.mean(values * values, axis=-1, keepdims=True) + EPSILON)


def contract_rows(left, right):
    return lax.dot_general(
        left, right, (((0,), (0,)), ((), ())), preferred_element_type=jnp.float32
    )


def contract_cols(left, right):
    return lax.dot_general(
        left, right, (((1,), (1,)), ((), ())), preferred_element_type=jnp.float32
    )


def per_device(
    teacher_in,
    teacher_gain,
    t_gate,
    t_up,
    t_down,
    student_in,
    student_gain,
    s_gate,
    s_up,
    s_down,
    proj,
    layer_map,
):
    tensor_count = lax.axis_size("tensor")
    tensor_pos = lax.axis_index("tensor")
    token_count = teacher_in.shape[0]
    own_rows = token_count // tensor_count
    row_start = tensor_pos * own_rows
    state = teacher_in
    own_states = []
    full_states = []
    for k in range(T_LAYERS):
        state_wide = state.astype(jnp.float32)
        normed = (state_wide * inverse_rms(state_wide) * teacher_gain[k]).astype(jnp.bfloat16)
        gate_act = jnp.dot(
            normed,
            lax.all_gather(t_gate[k], "dp", axis=0, tiled=True),
            preferred_element_type=jnp.float32,
        )
        up_act = jnp.dot(
            normed,
            lax.all_gather(t_up[k], "dp", axis=0, tiled=True),
            preferred_element_type=jnp.float32,
        )
        hidden = (jax.nn.silu(gate_act) * up_act).astype(jnp.bfloat16)
        down_full = lax.all_gather(t_down[k], "dp", axis=1, tiled=True)
        summed = lax.psum(
            jnp.dot(hidden, down_full, preferred_element_type=jnp.float32).astype(jnp.bfloat16),
            "tensor",
        ).astype(jnp.float32)
        state = (state_wide + summed).astype(jnp.bfloat16)
        own_new = lax.dynamic_slice_in_dim(state, row_start, own_rows, 0)
        own_states.append(own_new)
        full_states.append(state)
    col_width = proj.shape[1]
    col_start = tensor_pos * col_width
    targets = jnp.stack(
        [lax.dynamic_slice_in_dim(full, col_start, col_width, 1) for full in full_states]
    )
    states = [student_in]
    normeds, gates, ups, units, scales = ([], [], [], [], [])
    for l in range(S_LAYERS):
        wide = states[l].astype(jnp.float32)
        scale = inverse_rms(wide)
        normed = (wide * scale * student_gain[l]).astype(jnp.bfloat16)
        gate_act = jnp.dot(normed, s_gate[l], preferred_element_type=jnp.float32)
        up_act = jnp.dot(normed, s_up[l], preferred_element_type=jnp.float32)
        units_now = (jax.nn.silu(gate_act) * up_act).astype(jnp.bfloat16)
        down_now = s_down[l]
        student_part = lax.psum_scatter(
            jnp.dot(units_now, down_now, preferred_element_type=jnp.float32).astype(jnp.bfloat16),
            "tensor",
            scatter_dimension=0,
            tiled=True,
        ).astype(jnp.float32)
        own_wide = lax.dynamic_slice_in_dim(wide, row_start, own_rows, 0)
        own_next = (own_wide + student_part).astype(jnp.bfloat16)
        states.append(lax.all_gather(own_next, "tensor", axis=0, tiled=True))
        normeds.append(normed)
        gates.append(gate_act)
        ups.append(up_act)
        units.append(units_now)
        scales.append(scale)
    error_parts = []
    deltas = []
    for l in range(S_LAYERS):
        predicted = jnp.dot(states[l + 1], proj, preferred_element_type=jnp.float32)
        target = lax.dynamic_index_in_dim(targets, layer_map[l], 0, keepdims=False).astype(
            jnp.float32
        )
        errors = predicted - target
        error_parts.append(jnp.sum(errors * errors))
        deltas.append((errors * (2.0 / (S_LAYERS * SEQ))).astype(jnp.bfloat16))
    error_local = jnp.stack(error_parts)
    error_total = lax.psum(error_local, ("dp", "tensor"))
    grad_x = lax.psum(
        contract_cols(deltas[S_LAYERS - 1], proj).astype(jnp.bfloat16), "tensor"
    ).astype(jnp.float32)
    gate_grads = [None] * S_LAYERS
    up_grads = [None] * S_LAYERS
    down_grads = [None] * S_LAYERS
    for l in reversed(range(S_LAYERS)):
        grad_out = grad_x.astype(jnp.bfloat16)
        grad_units = contract_cols(grad_out, s_down[l])
        sigma = jax.nn.sigmoid(gates[l])
        grad_gate_act = (grad_units * ups[l] * sigma * (1.0 + gates[l] * (1.0 - sigma))).astype(
            jnp.bfloat16
        )
        grad_up_act = (grad_units * jax.nn.silu(gates[l])).astype(jnp.bfloat16)
        gate_grads[l] = contract_rows(normeds[l], grad_gate_act)
        up_grads[l] = contract_rows(normeds[l], grad_up_act)
        down_grads[l] = contract_rows(units[l], grad_out)
        if l > 0:
            norm_part = contract_cols(grad_gate_act, s_gate[l]) + contract_cols(
                grad_up_act, s_up[l]
            )
            proj_part = contract_cols(deltas[l - 1], proj)
            grad_norm, grad_side = (
                lax.psum(norm_part.astype(jnp.bfloat16), "tensor").astype(jnp.float32),
                lax.psum(proj_part.astype(jnp.bfloat16), "tensor").astype(jnp.float32),
            )
            wide = states[l].astype(jnp.float32)
            scaled = grad_norm * student_gain[l]
            through = scales[l] * scaled - wide * scales[l] ** 3 * jnp.mean(
                wide * scaled, axis=-1, keepdims=True
            )
            grad_x = grad_x + through + grad_side
    proj_local = contract_rows(states[1], deltas[0])
    l = 1
    proj_local = proj_local + contract_rows(states[l + 1], deltas[l])
    grad_gate, grad_up, grad_down, grad_proj = (
        lax.psum_scatter(
            jnp.stack(gate_grads).astype(jnp.bfloat16), "dp", scatter_dimension=1, tiled=True
        ).astype(jnp.float32),
        lax.psum_scatter(
            jnp.stack(up_grads).astype(jnp.bfloat16), "dp", scatter_dimension=1, tiled=True
        ).astype(jnp.float32),
        lax.psum_scatter(
            jnp.stack(down_grads).astype(jnp.bfloat16), "dp", scatter_dimension=2, tiled=True
        ).astype(jnp.float32),
        lax.psum_scatter(
            proj_local.astype(jnp.bfloat16), "dp", scatter_dimension=0, tiled=True
        ).astype(jnp.float32),
    )
    squares = jnp.stack(
        [
            jnp.sum(grad_gate * grad_gate),
            jnp.sum(grad_up * grad_up),
            jnp.sum(grad_down * grad_down),
            jnp.sum(grad_proj * grad_proj),
        ]
    )
    square_total = lax.psum(squares, ("dp", "tensor"))
    counts = jnp.array(
        [S_LAYERS * DS * FS, S_LAYERS * DS * FS, S_LAYERS * DS * FS, DS * DT], jnp.float32
    )
    mean_error = error_total / (token_count * lax.axis_size("dp") * DT)
    grad_rms = jnp.sqrt(square_total / counts)
    return (jnp.stack(own_states), grad_gate, grad_up, grad_down, grad_proj, mean_error, grad_rms)


def solution(mesh):
    return jax.shard_map(
        per_device,
        mesh=mesh,
        in_specs=(
            P("dp", None),
            P(),
            P(None, "dp", "tensor"),
            P(None, "dp", "tensor"),
            P(None, "tensor", "dp"),
            P("dp", None),
            P(),
            P(None, None, "tensor"),
            P(None, None, "tensor"),
            P(None, "tensor", None),
            P(None, "tensor"),
            P(),
        ),
        out_specs=(
            P(None, ("dp", "tensor"), None),
            P(None, "dp", "tensor"),
            P(None, "dp", "tensor"),
            P(None, "tensor", "dp"),
            P("dp", "tensor"),
            P(),
            P(),
        ),
        check_vma=False,
    )
```

profile of v0, /device:TPU:0, one launch (start us, length us, event | category | flops | bytes accessed | tf_op | source)
XLA Modules:
  0.0 709.6 jit_solution(3058975793029169596)
XLA Ops:
  8.1 2.7 fusion.110
  10.8 1.2 fusion.111
  12.1 2.5 fusion.112
  14.9 2.5 fusion.56
  17.7 1.8 multiply_convert_fusion.6
  21.0 1.5 fusion.71
  23.0 34.2 %all-gather.13.cloned.1.call-done = bf16[1,2048,1368]{1,2,0:T(8,128)(2,1)} async-done(((bf16[1,256,1368]{1,2,0:T(8,128)(2,1)}), bf16[1,2048,1368]{1,2,0:T(8,128)(2,1)}) %all-gather.13.cloned.1.call-update) | async-done | bytes 5603344 | tf_op jit(solution)/shard_map/all_gather | solution.py:58
  57.2 5.5 fusion.10
  62.6 40.5 %all-gather.15.cloned.1.call-done = bf16[1,2048,1368]{1,2,0:T(8,128)(2,1)} async-done(((bf16[1,256,1368]{1,2,0:T(8,128)(2,1)}), bf16[1,2048,1368]{1,2,0:T(8,128)(2,1)}) %all-gather.15.cloned.1.call-update) | async-done | bytes 5603344 | tf_op jit(solution)/shard_map/all_gather | solution.py:63
  103.2 46.0 %all-gather.17.cloned.1.call-done = bf16[1,1368,2048]{2,1,0:T(8,128)(2,1)} async-done(((bf16[1,1368,256]{2,1,0:T(8,128)(2,1)}), bf16[1,1368,2048]{2,1,0:T(8,128)(2,1)}) %all-gather.17.cloned.1.call-update) | async-done | bytes 5603344 | tf_op jit(solution)/shard_map/all_gather | solution.py:67
  149.2 11.8 %fusion.24 = bf16[256,2048]{1,0:T(8,128)(2,1)} fusion(bf16[1,1368,2048]{2,1,0:T(8,128)(2,1)} %all-gather.17.cloned.1.call-done, bf16[1,2048,1368]{1,2,0:T(8,128)(2,1)} %all-gather.15.cloned.1.call-done, f32[256,1368]{0,1:T(8,128)} %fusion.10, bf16[256,2048]{1,0:T(8,128)(2,1)S(1)} %copy-done.3, f32[2048]{0:T(1024)S(1)} %bitcast.152, f32[256]{0:T(256)S(1)} %add_rsqrt_fusion.3), kind=kOutput, calls=%fused_computation.25 | convolution fusion | flops 2873626624 | bytes 14713856 | tf_op jit(solution)/shard_map/dot_general | solution.py:69
  163.0 0.9 add_convert_fusion.3
  164.0 23.2 %all_gather.30 = bf16[256,1024]{1,0:T(8,128)(2,1)S(1)} all-gather(bf16[64,1024]{1,0:T(8,128)(2,1)S(1)} %add_convert_fusion.3), channel_id=1, replica_groups=mesh['dp'=8,'tensor'=4] {'tensor'}, dimensions={0}, use_global_device_ids=true | all-gather | bytes 655360 | tf_op jit(solution)/shard_map/all_gather | solution.py:99
  187.4 2.6 fusion.48
  190.6 1.9 multiply_convert_fusion.4
  193.7 1.5 fusion.74
  195.3 25.4 %all-reduce.7.cloned.1.call-done = bf16[256,2048]{1,0:T(8,128)(2,1)} async-done(((bf16[256,2048]{1,0:T(8,128)(2,1)}), bf16[256,2048]{1,0:T(8,128)(2,1)}) %all-reduce.7.cloned.1.call-update) | async-done | bytes 1048592 | tf_op jit(solution)/shard_map/psum | solution.py:68
  220.7 2.0 fusion.34
  222.8 5.5 fusion.4
  228.2 24.1 %all-gather.21.cloned.1.call-done = bf16[1,2048,1368]{1,2,0:T(8,128)(2,1)} async-done(((bf16[1,256,1368]{1,2,0:T(8,128)(2,1)}), bf16[1,2048,1368]{1,2,0:T(8,128)(2,1)}) %all-gather.21.cloned.1.call-update) | async-done | bytes 5603344 | tf_op jit(solution)/shard_map/all_gather | solution.py:63
  252.3 45.3 %all-gather.23.cloned.1.call-done = bf16[1,1368,2048]{2,1,0:T(8,128)(2,1)} async-done(((bf16[1,1368,256]{2,1,0:T(8,128)(2,1)}), bf16[1,1368,2048]{2,1,0:T(8,128)(2,1)}) %all-gather.23.cloned.1.call-update) | async-done | bytes 5603344 | tf_op jit(solution)/shard_map/all_gather | solution.py:67
  297.6 11.8 %fusion.27 = bf16[256,2048]{1,0:T(8,128)(2,1)} fusion(bf16[1,1368,2048]{2,1,0:T(8,128)(2,1)} %all-gather.23.cloned.1.call-done, bf16[1,2048,1368]{1,2,0:T(8,128)(2,1)} %all-gather.21.cloned.1.call-done, f32[256,1368]{0,1:T(8,128)} %fusion.4, bf16[256,2048]{1,0:T(8,128)(2,1)S(1)} %get-tuple-element.20, f32[2048]{0:T(1024)S(1)} %bitcast.150, ...), kind=kOutput, calls=%fused_computation.26 | convolution fusion | flops 2873626624 | bytes 14713856 | tf_op jit(solution)/shard_map/dot_general | solution.py:69
  314.0 1.1 convert_element_type.161
  315.1 1.1 add_convert_fusion.2
  316.2 22.9 %all_gather.31 = bf16[256,1024]{1,0:T(8,128)(2,1)} all-gather(bf16[64,1024]{1,0:T(8,128)(2,1)S(1)} %add_convert_fusion.2), channel_id=1, replica_groups=mesh['dp'=8,'tensor'=4] {'tensor'}, dimensions={0}, use_global_device_ids=true | all-gather | bytes 655360 | tf_op jit(solution)/shard_map/all_gather | solution.py:99
  339.1 30.7 %all-reduce.9.cloned.1.call-done = bf16[256,2048]{1,0:T(8,128)(2,1)} async-done(((bf16[256,2048]{1,0:T(8,128)(2,1)}), bf16[256,2048]{1,0:T(8,128)(2,1)}) %all-reduce.9.cloned.1.call-update) | async-done | bytes 1048592 | tf_op jit(solution)/shard_map/psum | solution.py:68
  369.8 1.7 fusion.37
  371.5 1.0 copy-done.4
  372.5 1.1 multiply_reduce_fusion.6
  374.4 1.3 convolution_convert_fusion.1
  375.9 2.1 multiply_reduce_fusion.7
  378.8 1.3 convolution_convert_fusion
  380.1 33.7 %all-reduce.11.cloned.1.call-done = bf16[256,1024]{1,0:T(8,128)(2,1)} async-done(((bf16[256,1024]{1,0:T(8,128)(2,1)}), bf16[256,1024]{1,0:T(8,128)(2,1)}) %all-reduce.11.cloned.1.call-update) | async-done | bytes 524304 | tf_op jit(solution)/shard_map/psum | solution.py:117
  413.8 3.5 multiply_convert_fusion.2
  418.1 0.9 copy-done.28
  419.0 1.5 fusion.77
  421.8 1.5 add_convert_fusion
  423.3 3.1 convert_bitcast_fusion
  426.5 45.5 %all-reduce.13.cloned.1.call-done = (bf16[256,1024]{1,0:T(8,128)(2,1)}, bf16[256,1024]{1,0:T(8,128)(2,1)}) async-done(((bf16[256,1024]{1,0:T(8,128)(2,1)}, bf16[256,1024]{1,0:T(8,128)(2,1)}), (bf16[256,1024]{1,0:T(8,128)(2,1)}, bf16[256,1024]{1,0:T(8,128)(2,1)})) %all-reduce.13.cloned.1.call-update) | async-done | bytes 1048592 | tf_op jit(solution)/shard_map/psum | solution.py:141
  472.0 1.3 multiply_reduce_fusion.3
  473.4 1.6 add_convert_fusion.1
  476.6 2.3 pad_maximum_fusion.2
  478.9 11.3 %copy.20 = bf16[2,1024,1024]{1,0,2:T(2,128)(2,1)} copy(bf16[2,1024,1024]{2,1,0:T(8,128)(2,1)} %pad_maximum_fusion.2) | data formatting | bytes 8388608
  490.2 5.6 copy.22
  495.9 1.0 copy-done.20
  497.7 2.4 fusion.50
  500.1 1.0 copy-done.32
  501.1 0.9 convert_bitcast_fusion.3
  502.0 2.3 pad_maximum_fusion.1
  507.6 1.0 convert_bitcast_fusion.5
  508.6 2.3 pad_maximum_fusion
  511.0 1.4 pad_maximum_fusion.4
  512.3 1.0 dynamic-slice_bitcast_fusion.2
  513.3 2.3 multiply_reduce_fusion.8
  515.6 30.8 %reduce-scatter.19.cloned.1.call-done = bf16[128,2048]{1,0:T(8,128)(2,1)} async-done(((bf16[1024,2048]{1,0:T(8,128)(2,1)}), bf16[128,2048]{1,0:T(8,128)(2,1)}) %reduce-scatter.19.cloned.1.call-update) | async-done | bytes 524304
  546.4 1.4 reshape.69
  548.4 1.8 multiply_reduce_fusion
  550.2 50.8 %reduce-scatter.15.cloned.1.call-done = bf16[2,128,1024]{2,1,0:T(8,128)(2,1)} async-done(((bf16[2,1024,1024]{2,1,0:T(8,128)(2,1)}), bf16[2,128,1024]{2,1,0:T(8,128)(2,1)}) %reduce-scatter.15.cloned.1.call-update) | async-done | bytes 524304 | tf_op jit(solution)/shard_map/reduce_scatter | solution.py:156
  601.0 2.8 multiply_reduce_fusion.1
  603.8 51.5 %reduce-scatter.13.cloned.1.call-done = bf16[2,128,1024]{2,1,0:T(8,128)(2,1)} async-done(((bf16[2,1024,1024]{2,1,0:T(8,128)(2,1)}), bf16[2,128,1024]{2,1,0:T(8,128)(2,1)}) %reduce-scatter.13.cloned.1.call-update) | async-done | bytes 524304 | tf_op jit(solution)/shard_map/reduce_scatter | solution.py:153
  655.3 2.8 multiply_reduce_fusion.2
  658.1 2.6 pad_maximum_fusion.5
  660.8 0.8 pad_maximum_fusion.3
  661.6 39.2 %all-reduce = (f32[2]{0:T(128)S(1)}, f32[4]{0:T(128)S(1)}) all-reduce(f32[2]{0:T(128)S(1)} %pad_maximum_fusion.4, f32[4]{0:T(128)S(1)} %pad_maximum_fusion.5), channel_id=1, replica_groups=mesh['dp'=8,'tensor'=4] {'dp','tensor'}, use_global_device_ids=true, to_apply=%region_18.19 | all-reduce | flops 6 | bytes 48 | tf_op jit(solution)/shard_map/psum | solution.py:116
  (133 shorter events, 18.6 us)
Async XLA Ops:
  8.0 364.4 %copy-start = (bf16[1024,512]{1,0:T(8,128)(2,1)S(1)}, bf16[1024,512]{1,0:T(8,128)(2,1)}, u32[]{:S(2)}) copy-start(bf16[1024,512]{1,0:T(8,128)(2,1)} %param.23) | copy-start | bytes 3145732
  8.0 2.8 copy-start.13
  8.0 49.1 %all-gather.13.cloned.1.call-start = ((), (), s32[]{:S(2)}) async-start(), calls=%async_computation.14 | async-start | bytes 6303744 | tf_op jit(solution)/shard_map/all_gather | solution.py:58
  10.7 92.4 %all-gather.15.cloned.1.call-start = ((), (), s32[]{:S(2)}) async-start(), calls=%async_computation.15 | async-start | bytes 6303744 | tf_op jit(solution)/shard_map/all_gather | solution.py:63
  12.0 2.7 copy-start.5
  12.0 2.9 copy-start.23
  12.0 137.2 %all-gather.17.cloned.1.call-start = ((), (), s32[]{:S(2)}) async-start(), calls=%async_computation.16 | async-start | bytes 6303744 | tf_op jit(solution)/shard_map/all_gather | solution.py:67
  14.6 148.4 %reduce-scatter.9.cloned.1.call-start = ((), (), s32[]{:S(2)}) async-start(), calls=%async_computation.8 | async-start | bytes 655360 | tf_op jit(solution)/shard_map/reduce_scatter | solution.py:91
  14.9 2.8 copy-start.25
  17.7 1.8 copy-start.34
  17.7 3.3 copy-start.29
  19.5 0.8 copy-start.14
  21.0 1.6 copy-start.22
  21.0 1.6 copy-start.3
  22.6 198.1 %all-reduce.7.cloned.1.call-start = ((), (), s32[]{:S(2)}) async-start(), calls=%async_computation.6 | async-start | bytes 2097152 | tf_op jit(solution)/shard_map/psum | solution.py:68
  161.1 61.7 %all-gather.19.cloned.1.call-start = ((), (), s32[]{:S(2)}) async-start(), calls=%async_computation.17 | async-start | bytes 6303744 | tf_op jit(solution)/shard_map/all_gather | solution.py:58
  161.7 90.7 %all-gather.21.cloned.1.call-start = ((), (), s32[]{:S(2)}) async-start(), calls=%async_computation.18 | async-start | bytes 6303744 | tf_op jit(solution)/shard_map/all_gather | solution.py:63
  162.2 135.4 %all-gather.23.cloned.1.call-start = ((), (), s32[]{:S(2)}) async-start(), calls=%async_computation.19 | async-start | bytes 6303744 | tf_op jit(solution)/shard_map/all_gather | solution.py:67
  162.8 152.3 %reduce-scatter.11.cloned.1.call-start = ((), (), s32[]{:S(2)}) async-start(), calls=%async_computation.9 | async-start | bytes 655360 | tf_op jit(solution)/shard_map/reduce_scatter | solution.py:91
  187.4 3.2 copy-start.26
  190.5 1.9 copy-start.37
  190.5 3.2 copy-start.30
  192.4 0.8 copy-start.16
  195.2 174.5 %all-reduce.9.cloned.1.call-start = ((), (), s32[]{:S(2)}) async-start(), calls=%async_computation.7 | async-start | bytes 2097152 | tf_op jit(solution)/shard_map/psum | solution.py:68
  228.2 81.3 %copy-start.24 = (s32[2]{0:T(128)S(1)}, s32[2]{0:T(128)}, u32[]{:S(2)}) copy-start(s32[2]{0:T(128)} %param.24) | copy-start | bytes 28
  309.5 104.3 %all-reduce.11.cloned.1.call-start = ((), (), s32[]{:S(2)}) async-start(), calls=%async_computation.10 | async-start | bytes 1048576 | tf_op jit(solution)/shard_map/psum | solution.py:117
  369.8 2.7 copy-start.9
  371.4 1.0 copy-start.4
  372.5 1.1 copy-start.21
  373.6 0.8 copy-start.11
  375.7 96.3 %all-reduce.13.cloned.1.call-start = ((), (), s32[]{:S(2)}) async-start(), calls=%async_computation.21 | async-start | bytes 2097152 | tf_op jit(solution)/shard_map/psum | solution.py:141
  378.0 0.8 copy-start.7
  413.8 3.6 copy-start.27
  413.8 5.3 copy-start.28
  417.2 0.9 copy-start.19
  417.3 3.3 copy-start.17
  419.0 1.6 copy-start.8
  420.6 1.0 copy-start.10
  420.6 92.7 %reduce-scatter.17.cloned.1.call-start = ((), (), s32[]{:S(2)}) async-start(), calls=%async_computation.13 | async-start | bytes 1179648 | tf_op jit(solution)/shard_map/reduce_scatter | solution.py:162
  420.7 1.1 copy-start.12
  421.8 1.5 copy-start.6
  423.3 123.2 %reduce-scatter.19.cloned.1.call-start = ((), (), s32[]{:S(2)}) async-start(), calls=%async_computation.20 | async-start | bytes 4718592
  472.0 3.0 copy-start.15
  475.0 1.6 copy-start.2
  495.8 1.0 copy-start.20
  495.9 105.1 %reduce-scatter.15.cloned.1.call-start = ((), (), s32[]{:S(2)}) async-start(), calls=%async_computation.12 | async-start | bytes 4718592 | tf_op jit(solution)/shard_map/reduce_scatter | solution.py:156
  497.7 3.4 copy-start.35
  500.1 1.0 copy-start.32
  504.4 1.1 copy-start.18
  504.4 150.9 %reduce-scatter.13.cloned.1.call-start = ((), (), s32[]{:S(2)}) async-start(), calls=%async_computation.11 | async-start | bytes 4718592 | tf_op jit(solution)/shard_map/reduce_scatter | solution.py:153
  505.5 1.3 copy-start.33
  505.5 1.8 copy-start.36
  505.5 2.2 copy-start.38
  548.4 153.5 %copy-start.1 = (bf16[1024,512]{1,0:T(8,128)(2,1)S(1)}, bf16[1024,512]{1,0:T(8,128)(2,1)}, u32[]{:S(2)}) copy-start(bf16[1024,512]{1,0:T(8,128)(2,1)} %param.23) | copy-start | bytes 3145732
  550.2 151.2 %copy-start.31 = (f32[4]{0:T(128)S(1)}, f32[4]{0:T(128)}, u32[]{:S(2)}) copy-start(f32[4]{0:T(128)} %constant.52) | copy-start | bytes 52
Sparse Core Ops, SparseCore 0:
  10.9 46.2 all-gather.12
  59.6 43.5 all-gather.14
  105.7 43.5 all-gather.16
  163.5 43.5 all-gather.18
  208.8 43.5 all-gather.20
  254.1 43.5 all-gather.22
  424.6 35.5 reduce-scatter.16
  496.0 50.4 reduce-scatter.18
  549.8 51.0 reduce-scatter.14
  604.2 51.0 reduce-scatter.12
Sparse Core Ops, SparseCore 1:
  22.6 24.6 reduce-scatter.8
  161.2 59.4 all-reduce.6
  223.4 21.1 reduce-scatter.10
  309.6 60.1 all-reduce.8
  375.8 37.9 all-reduce.10
  420.7 51.3 all-reduce.12
where the time goes:
time: 718 us; the launch traced here: 710 us
  waiting for transfers between devices  460 us (64%)
  blocking collectives  85.4 us (12%)
  matrix products  69.7 us (10%)
  local copies, waits for them, and re-layouts  39.6 us (6%)
  other arithmetic  33.1 us (5%)
  between operations  20.3 us (3%)
    all_gather x2, waiting for transfers between devices, per_device(): down_full = lax.all_gather(t_down[k], 'dp', axis=1, tiled=True)  91.3 us
    all_gather x2, waiting for transfers between devices, per_device(): lax.all_gather(t_up[k], 'dp', axis=0, tiled=True)  64.7 us
    psum x2, waiting for transfers between devices, per_device(): lax.psum(jnp.dot(hidden, down_full, preferred_element_type=jnp.float32).a...  56 us
    reduce_scatter x1, waiting for transfers between devices, per_device(): lax.psum_scatter(jnp.stack(gate_grads).astype(jnp.bfloat16), 'dp', scatte...  51.5 us
    reduce_scatter x1, waiting for transfers between devices, per_device(): lax.psum_scatter(jnp.stack(up_grads).astype(jnp.bfloat16), 'dp', scatter_...  50.8 us
    all_gather x2, blocking collectives, per_device(): states.append(lax.all_gather(own_next, 'tensor', axis=0, tiled=True))  46.1 us
    psum x1, waiting for transfers between devices, per_device(): lax.psum(proj_part.astype(jnp.bfloat16), 'tensor').astype(jnp.float32)  45.5 us
    psum x1, blocking collectives, per_device(): error_total = lax.psum(error_local, ('dp', 'tensor'))  39.2 us
  transfers between devices with their start and end apart: 16, of which 12 were waited for; matrix products, arithmetic and copies ran while one was open for 15% of the time, Pallas kernels for 0%

commit v1 on v0

--- a/solution.py
+++ b/solution.py
@@ -65,9 +65,12 @@
         )
         hidden = (jax.nn.silu(gate_act) * up_act).astype(jnp.bfloat16)
         down_full = lax.all_gather(t_down[k], "dp", axis=1, tiled=True)
-        summed = lax.psum(
-            jnp.dot(hidden, down_full, preferred_element_type=jnp.float32).astype(jnp.bfloat16),
-            "tensor",
+        summed = jnp.sum(
+            lax.all_gather(
+                jnp.dot(hidden, down_full, preferred_element_type=jnp.float32).astype(jnp.bfloat16),
+                "tensor",
+            ),
+            axis=0,
         ).astype(jnp.float32)
         state = (state_wide + summed).astype(jnp.bfloat16)
         own_new = lax.dynamic_slice_in_dim(state, row_start, own_rows, 0)

time: 718 us -> 842 us (1.17)
  waiting for transfers between devices: 460 us -> 579 us
  other arithmetic: 33.1 us -> 41.8 us
    all_gather x0 -> x2, waiting for transfers between devices: none -> 112 us  [per_device(): lax.all_gather(jnp.dot(hidden, down_full, preferred_element_type=jnp.floa...]
    psum x2 -> x0, waiting for transfers between devices: 56 us -> none  [per_device(): lax.psum(jnp.dot(hidden, down_full, preferred_element_type=jnp.float32).a...]
    all_gather x2, waiting for transfers between devices: 34.2 us -> 72.5 us  [per_device(): lax.all_gather(t_gate[k], 'dp', axis=0, tiled=True)]
    all_gather x2, waiting for transfers between devices: 64.7 us -> 91.4 us  [per_device(): lax.all_gather(t_up[k], 'dp', axis=0, tiled=True)]
    all_gather x2, waiting for transfers between devices: 91.3 us -> 80.4 us  [per_device(): down_full = lax.all_gather(t_down[k], 'dp', axis=1, tiled=True)]
    reduce_sum x0 -> x2, other arithmetic: none -> 8.5 us  [per_device(): jnp.sum(lax.all_gather(jnp.dot(hidden, down_full, preferred_element_type=...]
  transfers between devices with their start and end apart: 16 -> 16, of which waited for: 12 -> 14; matrix products, arithmetic and copies ran while one was open for 15% -> 14% of each run, Pallas kernels for 0% -> 0%
where the time goes in v1:
time: 842 us; the launch traced here: 834 us
  waiting for transfers between devices  579 us (69%)
  blocking collectives  82.6 us (10%)
  matrix products  69.7 us (8%)
  other arithmetic  41.8 us (5%)
  local copies, waits for them, and re-layouts  39.1 us (5%)
  between operations  20.4 us (2%)
    all_gather x2, waiting for transfers between devices, per_device(): lax.all_gather(jnp.dot(hidden, down_full, preferred_element_type=jnp.floa...  112 us
    all_gather x2, waiting for transfers between devices, per_device(): lax.all_gather(t_up[k], 'dp', axis=0, tiled=True)  91.4 us
    all_gather x2, waiting for transfers between devices, per_device(): down_full = lax.all_gather(t_down[k], 'dp', axis=1, tiled=True)  80.4 us
    all_gather x2, waiting for transfers between devices, per_device(): lax.all_gather(t_gate[k], 'dp', axis=0, tiled=True)  72.5 us
    reduce_scatter x1, waiting for transfers between devices, per_device(): lax.psum_scatter(jnp.stack(up_grads).astype(jnp.bfloat16), 'dp', scatter_...  51.7 us
    reduce_scatter x1, waiting for transfers between devices, per_device(): lax.psum_scatter(jnp.stack(gate_grads).astype(jnp.bfloat16), 'dp', scatte...  50.6 us
    psum x1, waiting for transfers between devices, per_device(): lax.psum(proj_part.astype(jnp.bfloat16), 'tensor').astype(jnp.float32)  45.5 us
    all_gather x2, blocking collectives, per_device(): states.append(lax.all_gather(own_next, 'tensor', axis=0, tiled=True))  43.4 us
  transfers between devices with their start and end apart: 16, of which 14 were waited for; matrix products, arithmetic and copies ran while one was open for 14% of the time, Pallas kernels for 0%

profile of v1, /device:TPU:0, one launch (start us, length us, event | category | flops | bytes accessed | tf_op | source)
XLA Modules:
  0.0 833.5 jit_solution(407378749247602792)
XLA Ops:
  8.1 2.7 fusion.110
  10.8 1.2 fusion.112
  12.1 2.5 fusion.111
  14.9 2.5 fusion.56
  17.8 1.8 multiply_convert_fusion.6
  19.6 1.5 copy-done.29
  21.1 1.5 fusion.71
  23.0 34.2 %all-gather.17.cloned.1.call-done = bf16[1,2048,1368]{1,2,0:T(8,128)(2,1)} async-done(((bf16[1,256,1368]{1,2,0:T(8,128)(2,1)}), bf16[1,2048,1368]{1,2,0:T(8,128)(2,1)}) %all-gather.17.cloned.1.call-update) | async-done | bytes 5603344 | tf_op jit(solution)/shard_map/all_gather | solution.py:58
  57.2 5.5 fusion.10
  62.7 40.5 %all-gather.21.cloned.1.call-done = bf16[1,1368,2048]{2,1,0:T(8,128)(2,1)} async-done(((bf16[1,1368,256]{2,1,0:T(8,128)(2,1)}), bf16[1,1368,2048]{2,1,0:T(8,128)(2,1)}) %all-gather.21.cloned.1.call-update) | async-done | bytes 5603344 | tf_op jit(solution)/shard_map/all_gather | solution.py:67
  103.2 46.0 %all-gather.19.cloned.1.call-done = bf16[1,2048,1368]{1,2,0:T(8,128)(2,1)} async-done(((bf16[1,256,1368]{1,2,0:T(8,128)(2,1)}), bf16[1,2048,1368]{1,2,0:T(8,128)(2,1)}) %all-gather.19.cloned.1.call-update) | async-done | bytes 5603344 | tf_op jit(solution)/shard_map/all_gather | solution.py:63
  149.3 11.8 %fusion.24 = bf16[256,2048]{1,0:T(8,128)(2,1)} fusion(bf16[1,1368,2048]{2,1,0:T(8,128)(2,1)} %all-gather.21.cloned.1.call-done, bf16[1,2048,1368]{1,2,0:T(8,128)(2,1)} %all-gather.19.cloned.1.call-done, f32[256,1368]{0,1:T(8,128)} %fusion.10, bf16[256,2048]{1,0:T(8,128)(2,1)S(1)} %copy-done.3, f32[2048]{0:T(1024)S(1)} %bitcast.156, f32[256]{0:T(256)S(1)} %add_rsqrt_fusion.3), kind=kOutput, calls=%fused_computation.25 | convolution fusion | flops 2873626624 | bytes 14713856 | tf_op jit(solution)/shard_map/dot_general | solution.py:70
  164.3 23.1 %all_gather.46 = bf16[256,1024]{1,0:T(8,128)(2,1)S(1)} all-gather(bf16[64,1024]{1,0:T(8,128)(2,1)S(1)} %add_convert_fusion.3), channel_id=1, replica_groups=mesh['dp'=8,'tensor'=4] {'tensor'}, dimensions={0}, use_global_device_ids=true | all-gather | bytes 655360 | tf_op jit(solution)/shard_map/all_gather | solution.py:102
  187.6 2.5 fusion.48
  190.5 1.8 multiply_convert_fusion.4
  192.3 1.3 copy-done.30
  193.7 1.5 fusion.74
  195.2 51.6 %all-gather.23.cloned.1.call-done = bf16[1024,2048]{1,0:T(8,128)(2,1)} async-done(((bf16[256,2048]{1,0:T(8,128)(2,1)}), bf16[1024,2048]{1,0:T(8,128)(2,1)}) %all-gather.23.cloned.1.call-update) | async-done | bytes 4194320 | tf_op jit(solution)/shard_map/all_gather | solution.py:69
  246.8 4.2 reduce_sum.124
  251.1 2.0 fusion.34
  253.1 38.3 %all-gather.25.cloned.1.call-done = bf16[1,2048,1368]{1,2,0:T(8,128)(2,1)} async-done(((bf16[1,256,1368]{1,2,0:T(8,128)(2,1)}), bf16[1,2048,1368]{1,2,0:T(8,128)(2,1)}) %all-gather.25.cloned.1.call-update) | async-done | bytes 5603344 | tf_op jit(solution)/shard_map/all_gather | solution.py:58
  291.4 5.5 fusion.4
  296.9 39.8 %all-gather.29.cloned.1.call-done = bf16[1,1368,2048]{2,1,0:T(8,128)(2,1)} async-done(((bf16[1,1368,256]{2,1,0:T(8,128)(2,1)}), bf16[1,1368,2048]{2,1,0:T(8,128)(2,1)}) %all-gather.29.cloned.1.call-update) | async-done | bytes 5603344 | tf_op jit(solution)/shard_map/all_gather | solution.py:67
  336.8 45.3 %all-gather.27.cloned.1.call-done = bf16[1,2048,1368]{1,2,0:T(8,128)(2,1)} async-done(((bf16[1,256,1368]{1,2,0:T(8,128)(2,1)}), bf16[1,2048,1368]{1,2,0:T(8,128)(2,1)}) %all-gather.27.cloned.1.call-update) | async-done | bytes 5603344 | tf_op jit(solution)/shard_map/all_gather | solution.py:63
  382.1 11.8 %fusion.27 = bf16[256,2048]{1,0:T(8,128)(2,1)} fusion(bf16[1,1368,2048]{2,1,0:T(8,128)(2,1)} %all-gather.29.cloned.1.call-done, bf16[1,2048,1368]{1,2,0:T(8,128)(2,1)} %all-gather.27.cloned.1.call-done, f32[256,1368]{0,1:T(8,128)} %fusion.4, bf16[256,2048]{1,0:T(8,128)(2,1)S(1)} %get-tuple-element.20, f32[2048]{0:T(1024)S(1)} %bitcast.154, ...), kind=kOutput, calls=%fused_computation.26 | convolution fusion | flops 2873626624 | bytes 14713856 | tf_op jit(solution)/shard_map/dot_general | solution.py:70
  398.5 1.1 convert_element_type.165
  399.6 7.1 reduce-scatter.11.cloned.1.call-done
  406.7 1.0 add_convert_fusion.2
  407.8 20.2 %all_gather.47 = bf16[256,1024]{1,0:T(8,128)(2,1)} all-gather(bf16[64,1024]{1,0:T(8,128)(2,1)S(1)} %add_convert_fusion.2), channel_id=1, replica_groups=mesh['dp'=8,'tensor'=4] {'tensor'}, dimensions={0}, use_global_device_ids=true | all-gather | bytes 655360 | tf_op jit(solution)/shard_map/all_gather | solution.py:102
  428.0 60.8 %all-gather.31.cloned.1.call-done = bf16[1024,2048]{1,0:T(8,128)(2,1)} async-done(((bf16[256,2048]{1,0:T(8,128)(2,1)}), bf16[1024,2048]{1,0:T(8,128)(2,1)}) %all-gather.31.cloned.1.call-update) | async-done | bytes 4194320 | tf_op jit(solution)/shard_map/all_gather | solution.py:69
  488.9 4.2 reduce_sum.126
  493.1 1.7 fusion.37
  495.8 1.1 multiply_reduce_fusion.6
  497.7 1.3 convolution_convert_fusion.1
  499.1 2.1 multiply_reduce_fusion.7
  502.0 1.3 convolution_convert_fusion
  503.3 34.3 %all-reduce.5.cloned.1.call-done = bf16[256,1024]{1,0:T(8,128)(2,1)} async-done(((bf16[256,1024]{1,0:T(8,128)(2,1)}), bf16[256,1024]{1,0:T(8,128)(2,1)}) %all-reduce.5.cloned.1.call-update) | async-done | bytes 524304 | tf_op jit(solution)/shard_map/psum | solution.py:120
  537.6 3.5 multiply_convert_fusion.2
  542.9 1.5 fusion.77
  545.6 1.4 add_convert_fusion
  547.2 3.1 convert_bitcast_fusion
  550.3 45.5 %all-reduce.7.cloned.1.call-done = (bf16[256,1024]{1,0:T(8,128)(2,1)}, bf16[256,1024]{1,0:T(8,128)(2,1)}) async-done(((bf16[256,1024]{1,0:T(8,128)(2,1)}, bf16[256,1024]{1,0:T(8,128)(2,1)}), (bf16[256,1024]{1,0:T(8,128)(2,1)}, bf16[256,1024]{1,0:T(8,128)(2,1)})) %all-reduce.7.cloned.1.call-update) | async-done | bytes 1048592 | tf_op jit(solution)/shard_map/psum | solution.py:144
  595.8 1.3 multiply_reduce_fusion.3
  597.2 1.6 add_convert_fusion.1
  600.5 2.3 pad_maximum_fusion.2
  602.8 11.3 %copy.20 = bf16[2,1024,1024]{1,0,2:T(2,128)(2,1)} copy(bf16[2,1024,1024]{2,1,0:T(8,128)(2,1)} %pad_maximum_fusion.2) | data formatting | bytes 8388608
  614.1 5.6 copy.22
  621.6 2.5 fusion.50
  625.0 1.0 convert_bitcast_fusion.5
  626.0 2.4 pad_maximum_fusion
  628.5 1.0 copy-done.18
  632.2 2.4 pad_maximum_fusion.1
  634.6 1.4 pad_maximum_fusion.4
  636.0 1.0 dynamic-slice_bitcast_fusion.2
  637.0 2.3 multiply_reduce_fusion.8
  639.2 31.1 %reduce-scatter.19.cloned.1.call-done = bf16[128,2048]{1,0:T(8,128)(2,1)} async-done(((bf16[1024,2048]{1,0:T(8,128)(2,1)}), bf16[128,2048]{1,0:T(8,128)(2,1)}) %reduce-scatter.19.cloned.1.call-update) | async-done | bytes 524304
  670.3 1.4 reshape.71
  672.3 1.8 multiply_reduce_fusion
  674.0 50.6 %reduce-scatter.13.cloned.1.call-done = bf16[2,128,1024]{2,1,0:T(8,128)(2,1)} async-done(((bf16[2,1024,1024]{2,1,0:T(8,128)(2,1)}), bf16[2,128,1024]{2,1,0:T(8,128)(2,1)}) %reduce-scatter.13.cloned.1.call-update) | async-done | bytes 524304 | tf_op jit(solution)/shard_map/reduce_scatter | solution.py:156
  724.6 2.8 multiply_reduce_fusion.2
  727.5 51.7 %reduce-scatter.15.cloned.1.call-done = bf16[2,128,1024]{2,1,0:T(8,128)(2,1)} async-done(((bf16[2,1024,1024]{2,1,0:T(8,128)(2,1)}), bf16[2,128,1024]{2,1,0:T(8,128)(2,1)}) %reduce-scatter.15.cloned.1.call-update) | async-done | bytes 524304 | tf_op jit(solution)/shard_map/reduce_scatter | solution.py:159
  779.1 2.8 multiply_reduce_fusion.1
  782.0 2.6 pad_maximum_fusion.5
  785.4 39.2 %all-reduce = (f32[2]{0:T(128)S(1)}, f32[4]{0:T(128)S(1)}) all-reduce(f32[2]{0:T(128)S(1)} %pad_maximum_fusion.4, f32[4]{0:T(128)S(1)} %pad_maximum_fusion.5), channel_id=1, replica_groups=mesh['dp'=8,'tensor'=4] {'dp','tensor'}, use_global_device_ids=true, to_apply=%region_18.19 | all-reduce | flops 6 | bytes 48 | tf_op jit(solution)/shard_map/psum | solution.py:119
  (135 shorter events, 20.8 us)
Async XLA Ops:
  8.0 487.8 %copy-start = (bf16[1024,512]{1,0:T(8,128)(2,1)S(1)}, bf16[1024,512]{1,0:T(8,128)(2,1)}, u32[]{:S(2)}) copy-start(bf16[1024,512]{1,0:T(8,128)(2,1)} %param.23) | copy-start | bytes 3145732
  8.0 2.8 copy-start.13
  8.0 49.2 %all-gather.17.cloned.1.call-start = ((), (), s32[]{:S(2)}) async-start(), calls=%async_computation.12 | async-start | bytes 6303744 | tf_op jit(solution)/shard_map/all_gather | solution.py:58
  10.8 92.4 %all-gather.21.cloned.1.call-start = ((), (), s32[]{:S(2)}) async-start(), calls=%async_computation.14 | async-start | bytes 6303744 | tf_op jit(solution)/shard_map/all_gather | solution.py:67
  12.0 2.7 copy-start.5
  12.0 2.9 copy-start.23
  12.0 137.2 %all-gather.19.cloned.1.call-start = ((), (), s32[]{:S(2)}) async-start(), calls=%async_computation.13 | async-start | bytes 6303744 | tf_op jit(solution)/shard_map/all_gather | solution.py:63
  14.7 148.7 %reduce-scatter.9.cloned.1.call-start = ((), (), s32[]{:S(2)}) async-start(), calls=%async_computation.6 | async-start | bytes 655360 | tf_op jit(solution)/shard_map/reduce_scatter | solution.py:94
  14.9 2.8 copy-start.25
  17.8 1.8 copy-start.34
  17.8 3.3 copy-start.29
  19.6 3.0 copy-start.14
  21.1 1.6 copy-start.22
  21.1 1.6 copy-start.3
  22.6 224.2 %all-gather.23.cloned.1.call-start = ((), (), s32[]{:S(2)}) async-start(), calls=%async_computation.15 | async-start | bytes 5242880 | tf_op jit(solution)/shard_map/all_gather | solution.py:69
  161.1 130.3 %all-gather.25.cloned.1.call-start = ((), (), s32[]{:S(2)}) async-start(), calls=%async_computation.16 | async-start | bytes 6303744 | tf_op jit(solution)/shard_map/all_gather | solution.py:58
  161.7 175.1 %all-gather.29.cloned.1.call-start = ((), (), s32[]{:S(2)}) async-start(), calls=%async_computation.18 | async-start | bytes 6303744 | tf_op jit(solution)/shard_map/all_gather | solution.py:67
  162.4 219.7 %all-gather.27.cloned.1.call-start = ((), (), s32[]{:S(2)}) async-start(), calls=%async_computation.17 | async-start | bytes 6303744 | tf_op jit(solution)/shard_map/all_gather | solution.py:63
  163.2 243.5 %reduce-scatter.11.cloned.1.call-start = ((), (), s32[]{:S(2)}) async-start(), calls=%async_computation.7 | async-start | bytes 655360 | tf_op jit(solution)/shard_map/reduce_scatter | solution.py:94
  187.6 2.9 copy-start.26
  190.5 1.8 copy-start.37
  190.5 3.2 copy-start.30
  192.3 2.8 copy-start.16
  195.2 293.7 %all-gather.31.cloned.1.call-start = ((), (), s32[]{:S(2)}) async-start(), calls=%async_computation.19 | async-start | bytes 5242880 | tf_op jit(solution)/shard_map/all_gather | solution.py:69
  296.9 97.1 %copy-start.24 = (s32[2]{0:T(128)S(1)}, s32[2]{0:T(128)}, u32[]{:S(2)}) copy-start(s32[2]{0:T(128)} %param.24) | copy-start | bytes 28
  394.0 143.6 %all-reduce.5.cloned.1.call-start = ((), (), s32[]{:S(2)}) async-start(), calls=%async_computation.8 | async-start | bytes 1048576 | tf_op jit(solution)/shard_map/psum | solution.py:120
  493.1 2.7 copy-start.9
  494.8 1.0 copy-start.4
  495.8 1.1 copy-start.21
  497.0 0.8 copy-start.11
  499.0 96.8 %all-reduce.7.cloned.1.call-start = ((), (), s32[]{:S(2)}) async-start(), calls=%async_computation.21 | async-start | bytes 2097152 | tf_op jit(solution)/shard_map/psum | solution.py:144
  501.2 0.8 copy-start.7
  537.6 3.6 copy-start.27
  537.6 5.3 copy-start.28
  541.1 0.9 copy-start.17
  541.1 3.3 copy-start.19
  542.9 1.6 copy-start.8
  544.4 1.0 copy-start.10
  544.4 92.5 %reduce-scatter.17.cloned.1.call-start = ((), (), s32[]{:S(2)}) async-start(), calls=%async_computation.11 | async-start | bytes 1179648 | tf_op jit(solution)/shard_map/reduce_scatter | solution.py:165
  544.5 1.1 copy-start.12
  545.6 1.5 copy-start.6
  547.1 123.2 %reduce-scatter.19.cloned.1.call-start = ((), (), s32[]{:S(2)}) async-start(), calls=%async_computation.20 | async-start | bytes 4718592
  595.8 3.0 copy-start.15
  598.9 1.6 copy-start.2
  619.7 1.0 copy-start.20
  619.7 104.9 %reduce-scatter.13.cloned.1.call-start = ((), (), s32[]{:S(2)}) async-start(), calls=%async_computation.9 | async-start | bytes 4718592 | tf_op jit(solution)/shard_map/reduce_scatter | solution.py:156
  621.5 3.5 copy-start.35
  621.6 3.5 copy-start.38
  624.1 1.0 copy-start.32
  628.4 1.1 copy-start.18
  628.5 150.7 %reduce-scatter.15.cloned.1.call-start = ((), (), s32[]{:S(2)}) async-start(), calls=%async_computation.10 | async-start | bytes 4718592 | tf_op jit(solution)/shard_map/reduce_scatter | solution.py:159
  629.5 1.3 copy-start.33
  629.5 1.7 copy-start.36
  672.3 153.4 %copy-start.1 = (bf16[1024,512]{1,0:T(8,128)(2,1)S(1)}, bf16[1024,512]{1,0:T(8,128)(2,1)}, u32[]{:S(2)}) copy-start(bf16[1024,512]{1,0:T(8,128)(2,1)} %param.23) | copy-start | bytes 3145732
  674.0 151.1 %copy-start.31 = (f32[4]{0:T(128)S(1)}, f32[4]{0:T(128)}, u32[]{:S(2)}) copy-start(f32[4]{0:T(128)} %constant.55) | copy-start | bytes 52
Sparse Core Ops, SparseCore 0:
  10.9 46.2 all-gather.16
  59.6 43.5 all-gather.20
  105.7 43.5 all-gather.18
  548.1 35.5 reduce-scatter.16
  619.8 50.4 reduce-scatter.18
  673.5 51.0 reduce-scatter.12
  728.0 51.0 reduce-scatter.14
Sparse Core Ops, SparseCore 1:
  22.7 24.6 reduce-scatter.8
  161.2 85.6 all-gather.22
  248.6 42.8 all-gather.24
  293.3 43.4 all-gather.28
  338.7 43.4 all-gather.26
  385.0 21.7 reduce-scatter.10
  408.7 80.1 all-gather.30
  499.1 38.4 all-reduce.4
  544.5 51.3 all-reduce.6
